TPU v7x, 32 devices: a whole 2x2x4 slice. The times are simulated.
32 devices in a mesh: ga: 2 (over core), band: 16 (over z, y, x).
Axes of the slice: x: 2, y: 2, z: 4, core: 2. Of those that a mesh axis runs over, the one named last changes fastest.
Arguments:
- orbitals: bfloat16 [1024, 2, 16384], P('band', None, 'ga'), may hold values from -6 to 6
- projectors: bfloat16 [864, 2, 16384], P(None, None, ('ga', 'band')), may hold values from -0.03125 to 0.03125
- coupling: float32 [4, 18, 18], replicated, may hold values from -6 to 6
- species: int32 [48], replicated, may hold values from 0 to 3
- offsets: int32 [48], replicated, may hold values from 0 to 846, as said below
Outputs:
- applied: bfloat16 [1024, 2, 16384], P('band', None, 'ga')
Inputs may be any that keep to these rules, and one draw needn't show every extreme that they name: Each atom's 18 projectors are the 18 consecutive rows of projectors starting at its offset; offsets are multiples of 18, and the atoms' blocks are distinct and cover all 864 rows.
All inputs are finite; a program needn't handle non-finite values.
Results may differ from a plain program's by a relative error of at most 0.0049.
Values may be sent and summed in bfloat16 or wider, within the bound.
A program may use at most 64 MiB of HBM per device.

v0:
```python
import jax
import jax.numpy as jnp
from jax import lax
from jax.sharding import PartitionSpec as P


def block_matrices(coupling, species, offsets):
    per_atom = coupling.shape[1]
    count = offsets.shape[0]
    blocks = jnp.arange(count, dtype=jnp.int32)
    matches = (offsets[None, :] == blocks[:, None] * per_atom).astype(jnp.int32)
    atom_kind = jnp.sum(matches * species[None, :], axis=1)
    onehot = (atom_kind[:, None] == jnp.arange(coupling.shape[0], dtype=jnp.int32)[None, :]).astype(
        jnp.float32
    )
    table = coupling.reshape(coupling.shape[0], per_atom * per_atom)
    picked = jnp.dot(
        onehot, table, precision=lax.Precision.HIGHEST, preferred_element_type=jnp.float32
    )
    return picked.reshape(count, per_atom, per_atom)


def apply_coupling(matrices, becp):
    count = matrices.shape[0]
    per_atom = matrices.shape[1]
    height = becp.shape[0]
    widths = becp.shape[2]
    blocked = becp.reshape(count, per_atom, 2 * widths)
    coupled = jnp.einsum("aij,ajc->aic", matrices, blocked, precision=lax.Precision.HIGHEST)
    return coupled.reshape(height, 2, widths).astype(jnp.bfloat16)


def project_bands(projectors, spread):
    total_proj = projectors.shape[0]
    total_bands = spread.shape[0]
    flat_proj = projectors.reshape(total_proj, -1)
    turned = jnp.concatenate([spread[:, 1, :], -spread[:, 0, :]], axis=1)
    stacked = jnp.concatenate([spread.reshape(total_bands, -1), turned], axis=0)
    partial_value = lax.dot_general(
        flat_proj, stacked, (((1,), (1,)), ((), ())), preferred_element_type=jnp.float32
    )
    return partial_value.reshape(total_proj, 2, total_bands)


def add_back(projectors, dbecp):
    total_proj = projectors.shape[0]
    total_bands = dbecp.shape[2]
    columns = dbecp.reshape(total_proj, 2 * total_bands)
    real_part = lax.dot_general(
        columns, projectors[:, 0, :], (((0,), (0,)), ((), ())), preferred_element_type=jnp.float32
    )
    imag_part = lax.dot_general(
        columns, projectors[:, 1, :], (((0,), (0,)), ((), ())), preferred_element_type=jnp.float32
    )
    out_real = real_part[:total_bands] - imag_part[total_bands:]
    out_imag = imag_part[:total_bands] + real_part[total_bands:]
    return jnp.stack([out_real, out_imag], axis=1).astype(jnp.bfloat16)


def per_device(orbitals, projectors, coupling, species, offsets):
    matrices = block_matrices(coupling, species, offsets)
    spread = lax.all_to_all(orbitals, "band", split_axis=2, concat_axis=0, tiled=True)
    partial_value = project_bands(projectors, spread)
    becp = lax.psum(partial_value, ("ga", "band"))
    dbecp = apply_coupling(matrices, becp)
    result = add_back(projectors, dbecp)
    return lax.all_to_all(result, "band", split_axis=0, concat_axis=2, tiled=True)


def solution(mesh):
    placed = (P("band", None, "ga"), P(None, None, ("ga", "band")), P(), P(), P())
    return jax.shard_map(
        per_device, mesh=mesh, in_specs=placed, out_specs=P("band", None, "ga"), check_vma=False
    )
```

profile of v0, /device:TPU:0, one launch (start us, length us, event | category | flops | bytes accessed | tf_op | source)
XLA Modules:
  0.0 417.0 jit_solution(8911082358564989493)
XLA Ops:
  6.5 11.4 %copy.45 = bf16[64,2,8192]{0,1,2:T(2,128)(2,1)} copy(bf16[64,2,8192]{2,1,0:T(2,128)(2,1)} %param.5) | data formatting | bytes 4194304 | tf_op args[0]
  17.9 7.5 %reshape.39 = bf16[16,2,32768]{2,1,0:T(2,128)(2,1)} reshape(bf16[8192,2,64]{2,1,0:T(2,128)(2,1)} %bitcast.46) | data formatting | bytes 4194304
  25.4 0.0 copy-start
  25.4 8.5 %all-to-all-start = ((bf16[16,2,32768]{2,1,0:T(2,128)(2,1)}), bf16[16,2,32768]{2,1,0:T(2,128)(2,1)}, u32[]{:S(2)}, u32[]{:S(2)}) async-start(bf16[16,2,32768]{2,1,0:T(2,128)(2,1)} %reshape.39), calls=%async_computation | async-start | bytes 4194304 | tf_op jit(solution)/shard_map/all_to_all | solution.py:62
  34.0 0.0 all-reduce.2.cloned.1.call-start
  34.0 0.0 copy-done
  34.0 0.5 copy.60
  34.5 42.6 %all-to-all-done = bf16[16,2,32768]{2,1,0:T(2,128)(2,1)} async-done(((bf16[16,2,32768]{2,1,0:T(2,128)(2,1)}), bf16[16,2,32768]{2,1,0:T(2,128)(2,1)}, u32[]{:S(2)}, u32[]{:S(2)}) %all-to-all-start) | async-done | bytes 2097184 | tf_op jit(solution)/shard_map/all_to_all | solution.py:62
  77.1 7.4 %reshape.40 = bf16[8192,2,64]{2,1,0:T(2,128)(2,1)} reshape(bf16[16,2,32768]{2,1,0:T(2,128)(2,1)} %all-to-all-done) | data formatting | bytes 4194304
  84.4 10.6 %copy.55 = bf16[64,2,16,512]{3,0,2,1:T(8,128)(2,1)} copy(bf16[64,2,16,512]{0,1,3,2:T(2,128)(2,1)} %bitcast.44) | data formatting | bytes 4194304 | tf_op jit(solution)/shard_map/all_to_all | solution.py:62
  95.0 7.4 %copy.54 = bf16[64,2,16,512]{3,2,0,1:T(8,128)(2,1)} copy(bf16[64,2,16,512]{0,1,3,2:T(2,128)(2,1)} %bitcast.45) | data formatting | bytes 4194304 | tf_op jit(solution)/shard_map/all_to_all | solution.py:62
  102.4 0.0 copy-start.1
  102.4 1.8 slice_bitcast_fusion
  104.2 0.4 copy-done.1
  104.6 2.2 copy.47
  106.8 0.6 copy.59
  107.4 12.5 %fusion.6 = f32[864,2048]{1,0:T(8,128)} fusion(bf16[864,1024]{1,0:T(8,128)(2,1)S(1)} %bitcast.53, bf16[1024,512]{1,0:T(8,128)(2,1)S(1)} %get-tuple-element.8, bf16[1024,512]{1,0:T(8,128)(2,1)S(1)} %get-tuple-element.7, bf16[1024,1024]{1,0:T(8,128)(2,1)S(1)} %bitcast.52), kind=kOutput, calls=%fused_computation.6 | convolution fusion | flops 3636461568 | bytes 13041664 | tf_op jit(solution)/shard_map/dot_general | solution.py:39
  119.9 7.9 %reshape.36 = f32[48,18,2048]{2,1,0:T(8,128)} reshape(f32[864,2048]{1,0:T(8,128)} %fusion.6) | data formatting | bytes 14155776 | tf_op jit(solution)/shard_map/reshape | solution.py:28
  127.8 0.0 copy-start.5
  127.8 0.0 copy-start.6
  127.8 0.0 copy-start.7
  127.8 0.0 all-reduce.2.cloned.1.call-update
  127.8 0.7 copy-done.5
  128.6 0.1 reshape.32
  128.6 0.1 dot_general.22
  128.8 0.0 copy-done.6
  128.8 0.0 copy-done.7
  128.8 0.2 select_reduce_fusion
  128.9 0.4 fusion.16
  129.4 0.3 copy.49
  129.7 4.2 %fusion.22 = (bf16[864,1,512]{2,1,0:T(2,128)(2,1)}, bf16[864,1,512]{2,1,0:T(2,128)(2,1)}) fusion(bf16[864,2,512]{2,1,0:T(2,128)(2,1)S(1)} %copy-done), kind=kLoop, calls=%fused_computation.30 | loop fusion | bytes 3538944 | tf_op jit(solution)/shard_map/slice | solution.py:53
  133.9 189.5 %all-reduce.2.cloned.1.call-done = f32[48,18,2048]{2,1,0:T(8,128)} async-done(((f32[48,18,2048]{2,1,0:T(8,128)}), f32[48,18,2048]{2,1,0:T(8,128)}) %all-reduce.2.cloned.1.call-update) | async-done | bytes 7077904 | tf_op jit(solution)/shard_map/psum | solution.py:64
  323.4 12.2 %convolution_convert_fusion = bf16[48,18,2048]{2,1,0:T(8,128)(2,1)} fusion(f32[48,18,18]{2,1,0:T(8,128)S(1)} %copy.49, f32[48,18,2048]{2,1,0:T(8,128)} %all-reduce.2.cloned.1.call-done), kind=kOutput, calls=%fused_computation.7 | convolution fusion | flops 383975424 | bytes 10679040 | tf_op jit(solution)/shard_map/aij,ajc->aic/dot_general | solution.py:29
  335.5 0.0 copy-start.4
  335.5 6.2 %convert_element_type.12 = bf16[864,2048]{1,0:T(8,128)(2,1)} reshape(bf16[48,18,2048]{2,1,0:T(8,128)(2,1)} %convolution_convert_fusion) | data formatting | bytes 7077888 | tf_op jit(solution)/shard_map/convert_element_type | solution.py:30
  341.7 0.0 copy-done.4
  341.7 0.0 copy-start.2
  341.7 0.0 copy-start.3
  341.8 4.6 %fusion.14 = f32[2048,512]{1,0:T(8,128)S(1)} fusion(bf16[864,2048]{1,0:T(8,128)(2,1)} %convert_element_type.12, bf16[864,1,512]{2,1,0:T(2,128)(2,1)S(1)} %copy-done.4), kind=kOutput, calls=%fused_computation.19 | convolution fusion | flops 1811939328 | bytes 8617984 | tf_op jit(solution)/shard_map/dot_general | solution.py:52
  346.3 0.0 copy-done.2
  346.4 0.0 copy-done.3
  346.4 2.4 fusion.15
  348.8 1.2 fusion.11
  350.0 0.2 pad_maximum_fusion
  350.2 2.2 copy.52
  352.4 54.2 %all_to_all.36 = bf16[1024,2,512]{2,1,0:T(2,128)(2,1)S(1)} all-to-all(bf16[1024,2,512]{2,1,0:T(2,128)(2,1)S(1)} %copy.52), channel_id=1, replica_groups=mesh['ga'=2,'band'=16] {'band'}, dimensions={0} | all-to-all | bytes 4194304 | tf_op jit(solution)/shard_map/all_to_all | solution.py:67
  406.5 3.6 copy.58
  (2 shorter events, 0.0 us)
Async XLA Ops:
  25.4 8.6 %copy-start = (bf16[864,2,512]{2,1,0:T(2,128)(2,1)S(1)}, bf16[864,2,512]{2,1,0:T(2,128)(2,1)}, u32[]{:S(2)}) copy-start(bf16[864,2,512]{2,1,0:T(2,128)(2,1)} %param.6) | copy-start | bytes 5308420
  25.4 51.6 %all-to-all-start = ((bf16[16,2,32768]{2,1,0:T(2,128)(2,1)}), bf16[16,2,32768]{2,1,0:T(2,128)(2,1)}, u32[]{:S(2)}, u32[]{:S(2)}) async-start(bf16[16,2,32768]{2,1,0:T(2,128)(2,1)} %reshape.39), calls=%async_computation | async-start | bytes 4194304 | tf_op jit(solution)/shard_map/all_to_all | solution.py:62
  34.0 289.4 %all-reduce.2.cloned.1.call-start = ((), (), s32[]{:S(2)}) async-start(), calls=%async_computation.2 | async-start | bytes 18874368 | tf_op jit(solution)/shard_map/psum | solution.py:64
  102.4 2.2 copy-start.1
  127.8 0.8 copy-start.5
  127.8 1.0 copy-start.6
  127.8 1.0 copy-start.7
  335.5 6.2 %copy-start.4 = (bf16[864,1,512]{2,1,0:T(2,128)(2,1)S(1)}, bf16[864,1,512]{2,1,0:T(2,128)(2,1)}, u32[]{:S(2)}) copy-start(bf16[864,1,512]{2,1,0:T(2,128)(2,1)} %get-tuple-element.9) | copy-start | bytes 2654212
  341.7 4.6 %copy-start.2 = (bf16[864,2048]{1,0:T(8,128)(2,1)S(1)}, bf16[864,2048]{1,0:T(8,128)(2,1)}, u32[]{:S(2)}) copy-start(bf16[864,2048]{1,0:T(8,128)(2,1)} %convert_element_type.12) | copy-start | bytes 10616836
  341.7 4.6 %copy-start.3 = (bf16[864,1,512]{2,1,0:T(2,128)(2,1)S(1)}, bf16[864,1,512]{2,1,0:T(2,128)(2,1)}, u32[]{:S(2)}) copy-start(bf16[864,1,512]{2,1,0:T(2,128)(2,1)} %get-tuple-element.10) | copy-start | bytes 2654212
Sparse Core Ops, SparseCore 0:
  127.9 195.3 all-reduce.1
where the time goes:
time: 419 us; the launch traced here: 417 us
  waiting for transfers between devices  232 us (55%)
  local copies, waits for them, and re-layouts  73.2 us (17%)
  blocking collectives  54.2 us (13%)
  matrix products  32 us (8%)
  between operations  13.6 us (3%)
  starting transfers between devices  8.57 us (2%)
    psum x1, waiting for transfers between devices, per_device(): becp = lax.psum(partial_value, ('ga', 'band'))  189 us
    all_to_all x1, blocking collectives, per_device(): lax.all_to_all(result, 'band', split_axis=0, concat_axis=2, tiled=True)  54.2 us
    all_to_all x1, waiting for transfers between devices, per_device(): lax.all_to_all(orbitals, 'band', split_axis=2, concat_axis=0, tiled=True)  42.6 us
    unnamed x22, local copies, waits for them, and re-layouts  28.5 us
    all_to_all x3, local copies, waits for them, and re-layouts, per_device(): lax.all_to_all(orbitals, 'band', split_axis=2, concat_axis=0, tiled=True)  20.1 us
    dot_general x1, matrix products, project_bands(): lax.dot_general(flat_proj, stacked, (((1,), (1,)), ((), ())), preferred_e...  12.5 us
    dot_general x1, matrix products, apply_coupling(): jnp.einsum('aij,ajc->aic', matrices, blocked, precision=lax.Precision.HIG...  12.2 us
    all_to_all x1, starting transfers between devices, per_device(): lax.all_to_all(orbitals, 'band', split_axis=2, concat_axis=0, tiled=True)  8.52 us
  transfers between devices with their start and end apart: 2, of which 2 were waited for; matrix products, arithmetic and copies ran while one was open for 1% of the time, Pallas kernels for 0%

commit v1 on v0

--- a/solution.py
+++ b/solution.py
@@ -61,7 +61,7 @@
     matrices = block_matrices(coupling, species, offsets)
     spread = lax.all_to_all(orbitals, "band", split_axis=2, concat_axis=0, tiled=True)
     partial_value = project_bands(projectors, spread)
-    becp = lax.psum(partial_value, ("ga", "band"))
+    becp = lax.psum(lax.psum(partial_value, "band"), "ga")
     dbecp = apply_coupling(matrices, becp)
     result = add_back(projectors, dbecp)
     return lax.all_to_all(result, "band", split_axis=0, concat_axis=2, tiled=True)

time: 419 us -> 510 us (1.22)
  waiting for transfers between devices: 232 us -> 308 us
  local copies, waits for them, and re-layouts: 73.2 us -> 86.9 us
    psum x1 -> x2, waiting for transfers between devices: 189 us -> 265 us  [per_device(): becp = lax.psum(lax.psum(partial_value, 'band'), 'ga')]
    reshape x0 -> x1, local copies, waits for them, and re-layouts: none -> 10.3 us  [project_bands(): return partial_value.reshape(total_proj, 2, total_bands)]
  transfers between devices with their start and end apart: 2 -> 3, of which waited for: 2 -> 3; matrix products, arithmetic and copies ran while one was open for 1% -> 1% of each run, Pallas kernels for 0% -> 0%
where the time goes in v1:
time: 510 us; the launch traced here: 508 us
  waiting for transfers between devices  308 us (60%)
  local copies, waits for them, and re-layouts  86.9 us (17%)
  blocking collectives  55.8 us (11%)
  matrix products  32 us (6%)
  between operations  13.6 us (3%)
  starting transfers between devices  8.79 us (2%)
    psum x2, waiting for transfers between devices, per_device(): becp = lax.psum(lax.psum(partial_value, 'band'), 'ga')  265 us
    all_to_all x1, blocking collectives, per_device(): lax.all_to_all(result, 'band', split_axis=0, concat_axis=2, tiled=True)  55.8 us
    all_to_all x1, waiting for transfers between devices, per_device(): lax.all_to_all(orbitals, 'band', split_axis=2, concat_axis=0, tiled=True)  42.6 us
    unnamed x22, local copies, waits for them, and re-layouts  28.5 us
    all_to_all x3, local copies, waits for them, and re-layouts, per_device(): lax.all_to_all(orbitals, 'band', split_axis=2, concat_axis=0, tiled=True)  20.1 us
    dot_general x1, matrix products, project_bands(): lax.dot_general(flat_proj, stacked, (((1,), (1,)), ((), ())), preferred_e...  12.5 us
    dot_general x1, matrix products, apply_coupling(): jnp.einsum('aij,ajc->aic', matrices, blocked, precision=lax.Precision.HIG...  12.2 us
    reshape x1, local copies, waits for them, and re-layouts, apply_coupling(): blocked = becp.reshape(count, per_atom, 2 * widths)  10.9 us
  transfers between devices with their start and end apart: 3, of which 3 were waited for; matrix products, arithmetic and copies ran while one was open for 1% of the time, Pallas kernels for 0%

profile of v1, /device:TPU:0, one launch (start us, length us, event | category | flops | bytes accessed | tf_op | source)
XLA Modules:
  0.0 508.1 jit_solution(11888097500540679888)
XLA Ops:
  6.5 11.4 %copy.45 = bf16[64,2,8192]{0,1,2:T(2,128)(2,1)} copy(bf16[64,2,8192]{2,1,0:T(2,128)(2,1)} %param.5) | data formatting | bytes 4194304 | tf_op args[0]
  17.9 7.5 %reshape.38 = bf16[16,2,32768]{2,1,0:T(2,128)(2,1)} reshape(bf16[8192,2,64]{2,1,0:T(2,128)(2,1)} %bitcast.46) | data formatting | bytes 4194304
  25.4 0.0 copy-start
  25.4 8.5 %all-to-all-start = ((bf16[16,2,32768]{2,1,0:T(2,128)(2,1)}), bf16[16,2,32768]{2,1,0:T(2,128)(2,1)}, u32[]{:S(2)}, u32[]{:S(2)}) async-start(bf16[16,2,32768]{2,1,0:T(2,128)(2,1)} %reshape.38), calls=%async_computation | async-start | bytes 4194304 | tf_op jit(solution)/shard_map/all_to_all | solution.py:62
  34.0 0.0 all-reduce.3.cloned.1.call-start
  34.0 0.0 copy-done
  34.0 0.5 copy.60
  34.5 42.6 %all-to-all-done = bf16[16,2,32768]{2,1,0:T(2,128)(2,1)} async-done(((bf16[16,2,32768]{2,1,0:T(2,128)(2,1)}), bf16[16,2,32768]{2,1,0:T(2,128)(2,1)}, u32[]{:S(2)}, u32[]{:S(2)}) %all-to-all-start) | async-done | bytes 2097184 | tf_op jit(solution)/shard_map/all_to_all | solution.py:62
  77.1 7.4 %reshape.39 = bf16[8192,2,64]{2,1,0:T(2,128)(2,1)} reshape(bf16[16,2,32768]{2,1,0:T(2,128)(2,1)} %all-to-all-done) | data formatting | bytes 4194304
  84.4 10.6 %copy.55 = bf16[64,2,16,512]{3,0,2,1:T(8,128)(2,1)} copy(bf16[64,2,16,512]{0,1,3,2:T(2,128)(2,1)} %bitcast.44) | data formatting | bytes 4194304 | tf_op jit(solution)/shard_map/all_to_all | solution.py:62
  95.0 7.4 %copy.54 = bf16[64,2,16,512]{3,2,0,1:T(8,128)(2,1)} copy(bf16[64,2,16,512]{0,1,3,2:T(2,128)(2,1)} %bitcast.45) | data formatting | bytes 4194304 | tf_op jit(solution)/shard_map/all_to_all | solution.py:62
  102.4 0.0 copy-start.1
  102.4 1.8 slice_bitcast_fusion
  104.2 0.4 copy-done.1
  104.6 2.2 copy.47
  106.8 0.6 copy.59
  107.4 12.5 %fusion.6 = f32[864,2048]{1,0:T(8,128)} fusion(bf16[864,1024]{1,0:T(8,128)(2,1)S(1)} %bitcast.53, bf16[1024,512]{1,0:T(8,128)(2,1)S(1)} %get-tuple-element.8, bf16[1024,512]{1,0:T(8,128)(2,1)S(1)} %get-tuple-element.7, bf16[1024,1024]{1,0:T(8,128)(2,1)S(1)} %bitcast.52), kind=kOutput, calls=%fused_computation.6 | convolution fusion | flops 3636461568 | bytes 13041664 | tf_op jit(solution)/shard_map/dot_general | solution.py:39
  119.9 10.3 %reshape.35 = f32[864,2,1024]{2,1,0:T(2,128)} reshape(f32[864,2048]{1,0:T(8,128)} %fusion.6) | data formatting | bytes 14155776 | tf_op jit(solution)/shard_map/reshape | solution.py:42
  130.2 0.0 all-reduce.3.cloned.1.call-update
  130.2 0.2 all-reduce.5.cloned.1.call-start
  130.5 231.1 %all-reduce.3.cloned.1.call-done = f32[864,2,1024]{2,1,0:T(2,128)} async-done(((f32[864,2,1024]{2,1,0:T(2,128)}), f32[864,2,1024]{2,1,0:T(2,128)}) %all-reduce.3.cloned.1.call-update) | async-done | bytes 7077904 | tf_op jit(solution)/shard_map/psum | solution.py:64
  361.6 10.9 %reshape.36 = f32[48,18,2048]{2,1,0:T(8,128)} reshape(f32[864,2,1024]{2,1,0:T(2,128)} %all-reduce.3.cloned.1.call-done) | data formatting | bytes 14155776 | tf_op jit(solution)/shard_map/reshape | solution.py:28
  372.5 0.0 copy-start.5
  372.5 0.0 copy-start.6
  372.5 0.0 copy-start.7
  372.5 0.0 all-reduce.5.cloned.1.call-update
  372.5 0.7 copy-done.5
  373.3 0.1 reshape.32
  373.4 0.1 dot_general.22
  373.5 0.0 copy-done.6
  373.5 0.0 copy-done.7
  373.5 0.2 select_reduce_fusion
  373.7 0.4 fusion.16
  374.1 0.3 copy.49
  374.4 4.5 fusion.22
  378.9 33.9 %all-reduce.5.cloned.1.call-done = f32[48,18,2048]{2,1,0:T(8,128)} async-done(((f32[48,18,2048]{2,1,0:T(8,128)}), f32[48,18,2048]{2,1,0:T(8,128)}) %all-reduce.5.cloned.1.call-update) | async-done | bytes 7077904 | tf_op jit(solution)/shard_map/psum | solution.py:64
  412.8 12.2 %convolution_convert_fusion = bf16[48,18,2048]{2,1,0:T(8,128)(2,1)} fusion(f32[48,18,18]{2,1,0:T(8,128)S(1)} %copy.49, f32[48,18,2048]{2,1,0:T(8,128)} %all-reduce.5.cloned.1.call-done), kind=kOutput, calls=%fused_computation.7 | convolution fusion | flops 383975424 | bytes 10679040 | tf_op jit(solution)/shard_map/aij,ajc->aic/dot_general | solution.py:29
  425.0 6.2 %convert_element_type.12 = bf16[864,2048]{1,0:T(8,128)(2,1)} reshape(bf16[48,18,2048]{2,1,0:T(8,128)(2,1)} %convolution_convert_fusion) | data formatting | bytes 7077888 | tf_op jit(solution)/shard_map/convert_element_type | solution.py:30
  431.2 0.0 copy-done.4
  431.2 4.6 fusion.14
  435.8 0.0 copy-done.2
  435.8 0.0 copy-done.3
  435.8 2.4 fusion.15
  438.2 1.2 fusion.11
  439.5 0.2 pad_maximum_fusion
  439.7 2.2 copy.52
  441.8 55.8 %all_to_all.36 = bf16[1024,2,512]{2,1,0:T(2,128)(2,1)S(1)} all-to-all(bf16[1024,2,512]{2,1,0:T(2,128)(2,1)S(1)} %copy.52), channel_id=1, replica_groups=mesh['ga'=2,'band'=16] {'band'}, dimensions={0} | all-to-all | bytes 4194304 | tf_op jit(solution)/shard_map/all_to_all | solution.py:67
  497.6 3.6 copy.58
  (5 shorter events, 0.0 us)
Async XLA Ops:
  25.4 8.6 %copy-start = (bf16[864,2,512]{2,1,0:T(2,128)(2,1)S(1)}, bf16[864,2,512]{2,1,0:T(2,128)(2,1)}, u32[]{:S(2)}) copy-start(bf16[864,2,512]{2,1,0:T(2,128)(2,1)} %param.6) | copy-start | bytes 5308420
  25.4 51.6 %all-to-all-start = ((bf16[16,2,32768]{2,1,0:T(2,128)(2,1)}), bf16[16,2,32768]{2,1,0:T(2,128)(2,1)}, u32[]{:S(2)}, u32[]{:S(2)}) async-start(bf16[16,2,32768]{2,1,0:T(2,128)(2,1)} %reshape.38), calls=%async_computation | async-start | bytes 4194304 | tf_op jit(solution)/shard_map/all_to_all | solution.py:62
  34.0 327.6 %all-reduce.3.cloned.1.call-start = ((), (), s32[]{:S(2)}) async-start(), calls=%async_computation.2 | async-start | bytes 14155776 | tf_op jit(solution)/shard_map/psum | solution.py:64
  102.4 2.2 copy-start.1
  130.2 282.6 %all-reduce.5.cloned.1.call-start = ((), (), s32[]{:S(2)}) async-start(), calls=%async_computation.3 | async-start | bytes 18874368 | tf_op jit(solution)/shard_map/psum | solution.py:64
  372.5 0.8 copy-start.5
  372.5 1.0 copy-start.6
  372.5 1.0 copy-start.7
  425.0 6.2 %copy-start.4 = (bf16[864,1,512]{2,1,0:T(2,128)(2,1)S(1)}, bf16[864,1,512]{2,1,0:T(2,128)(2,1)}, u32[]{:S(2)}) copy-start(bf16[864,1,512]{2,1,0:T(2,128)(2,1)} %get-tuple-element.9) | copy-start | bytes 2654212
  431.2 4.6 copy-start.2
  431.2 4.6 copy-start.3
Sparse Core Ops, SparseCore 0:
  130.4 231.1 all-reduce.2
  372.7 40.1 all-reduce.4
